TPU v7x, 32 devices: a 4x4x1 block of a 4x4x8 slice. The times are simulated.
32 devices in a mesh: rep: 1 (over z), data: 4 (over y), expert: 8 (over x, core).
Axes of the slice: x: 4, y: 4, z: 1, core: 2. Of those that a mesh axis runs over, the one named last changes fastest.
The devices are a block of a 4x4x8 slice.
Arguments:
- x: bfloat16 [32768, 2304], P(('rep', 'expert', 'data'))
- expert_idx: int32 [32768, 2], P(('rep', 'expert', 'data'))
- gate: float32 [32768, 2], P(('rep', 'expert', 'data'))
- w_gate: bfloat16 [8, 2304, 5760], P('expert', 'data')
- w_up: bfloat16 [8, 2304, 5760], P('expert', 'data')
- w_down: bfloat16 [8, 5760, 2304], P('expert', None, 'data')
Outputs:
- output: bfloat16 [32768, 2304], P(('rep', 'expert', 'data'))
All inputs are finite; a program needn't handle non-finite values.
Results may differ from a plain program's by a relative error of at most 0.001.
Values are sent between devices in bfloat16 or wider.
A program may use at most 768 MiB of HBM per device.

v0:
```python
import jax
import jax.numpy as jnp
from jax import lax
from jax.sharding import PartitionSpec as P


def capacity_rows(tok_rows, top_k, n_exp):
    return max(8, ((5 * top_k * tok_rows) // (4 * n_exp) + 7) // 8 * 8)


def slot_table(ids_flat, n_exp, n_group, capacity):
    n_local = n_exp // n_group
    one_hot = (ids_flat[:, None] == jnp.arange(n_exp, dtype=jnp.int32)[None, :]).astype(jnp.int32)
    slot_ids = jnp.sum((jnp.cumsum(one_hot, axis=0) - one_hot) * one_hot, axis=1)
    row_base = (ids_flat % n_local) * (n_group * capacity) + (ids_flat // n_local) * capacity
    return jnp.where(slot_ids < capacity, row_base + slot_ids, n_exp * capacity)


def dispatch_rows(x_loc, dest_row, n_slots, top_k):
    tok_rows = x_loc.shape[0]
    pair_token = jnp.arange(dest_row.shape[0], dtype=jnp.int32) // top_k
    src_tok = jnp.full((n_slots,), tok_rows, jnp.int32).at[dest_row].set(pair_token, mode="drop")
    return jnp.take(x_loc, src_tok, axis=0, mode="fill", fill_value=0)


def combine_rows(x_loc, gate_loc, back_rows, dest_row):
    tok_rows, d_model = x_loc.shape
    pair_out = jnp.take(back_rows, dest_row, axis=0, mode="fill", fill_value=0)
    mixed = jnp.sum(pair_out.reshape(tok_rows, gate_loc.shape[1], d_model) * gate_loc[:, :, None], axis=1)
    return (x_loc.astype(jnp.float32) + mixed).astype(jnp.bfloat16)


def expert_ffn(expert_rows, w_gate, w_up, w_down):
    gate_act = jnp.einsum("erd,edf->erf", expert_rows, w_gate, preferred_element_type=jnp.float32)
    up_act = jnp.einsum("erd,edf->erf", expert_rows, w_up, preferred_element_type=jnp.float32)
    hidden = (jax.nn.silu(gate_act) * up_act).astype(jnp.bfloat16)
    return jnp.einsum("erf,efd->erd", hidden, w_down, preferred_element_type=jnp.float32).astype(jnp.bfloat16)


def solution(mesh):
    n_group = mesh.shape["expert"]
    tok_spec = P(("rep", "expert", "data"), None)
    wide_spec = P("expert", "data", None)
    down_spec = P("expert", None, "data")

    def device_step(x_loc, idx_loc, gate_loc, wg_loc, wu_loc, wd_loc):
        tok_rows, d_model = x_loc.shape
        top_k = idx_loc.shape[1]
        n_local = wg_loc.shape[0]
        n_exp = n_local * n_group
        capacity = capacity_rows(tok_rows, top_k, n_exp)
        dest_row = slot_table(idx_loc.reshape(tok_rows * top_k), n_exp, n_group, capacity)
        send_rows = dispatch_rows(x_loc, dest_row, n_exp * capacity, top_k).reshape(n_local, n_group, capacity, d_model)
        recv_rows = lax.all_to_all(send_rows, "expert", 1, 1, tiled=True)
        wg_full = lax.all_gather(wg_loc, "data", axis=1, tiled=True)
        wu_full = lax.all_gather(wu_loc, "data", axis=1, tiled=True)
        wd_full = lax.all_gather(wd_loc, "data", axis=2, tiled=True)
        out_rows = expert_ffn(recv_rows.reshape(n_local, n_group * capacity, d_model), wg_full, wu_full, wd_full)
        back_rows = lax.all_to_all(out_rows.reshape(n_local, n_group, capacity, d_model), "expert", 1, 1, tiled=True)
        return combine_rows(x_loc, gate_loc, back_rows.reshape(n_exp * capacity, d_model), dest_row)

    return jax.shard_map(device_step, mesh=mesh, in_specs=(tok_spec, tok_spec, tok_spec, wide_spec, wide_spec, down_spec), out_specs=tok_spec, check_vma=False)
```

profile of v0, /device:TPU:100, one launch (start us, length us, event | category | flops | bytes accessed | tf_op | source)
XLA Modules:
  0.0 1036.9 jit_solution(7042879060892117799)
XLA Ops:
  6.5 0.0 copy-start.6
  6.5 0.0 all-gather.4.cloned.1.call-start
  6.6 0.7 all-gather.4.cloned.1.call-update
  7.3 0.1 all-gather.6.cloned.1.call-start
  7.4 0.7 all-gather.6.cloned.1.call-update
  8.1 0.0 copy-done.6
  8.1 0.2 copy.13
  8.4 0.0 copy-start
  8.4 0.3 eq.31
  8.6 0.3 eq.27
  8.9 2.3 reduce-window.6
  11.2 0.3 slice_reduce_fusion
  11.5 0.2 reduce-window.9
  11.7 0.3 mul.44
  12.0 0.1 add_bitcast_fusion
  12.2 0.0 copy-start.2
  12.2 0.6 copy-done.2
  12.8 0.0 copy-start.4
  12.8 8.1 scatter_custom_fusion
  20.8 0.1 broadcast_in_dim.34
  21.0 25.5 %gather_fusion = bf16[2560,2304]{1,0:T(8,128)(2,1)} fusion(bf16[1024,2304]{1,0:T(8,128)(2,1)} %param.6, s32[3072]{0:T(1024)S(1)} %pad_clamp_fusion), kind=kCustom, calls=%fused_computation | custom fusion | bytes 23603200 | tf_op jit(solution)/shard_map/jit(_take)/gather | solution.py:23
  46.5 0.0 copy-done
  46.5 0.0 copy-done.4
  46.5 10.4 broadcast_select_fusion.1
  56.8 6.1 all-to-all-start
  63.0 0.3 all-gather.8.cloned.1.call-start
  63.3 0.5 all-gather.8.cloned.1.call-update
  63.7 127.2 %all-to-all-done = bf16[1,8,320,2304]{3,2,0,1:T(8,128)(2,1)} async-done(((bf16[1,8,320,2304]{3,2,0,1:T(8,128)(2,1)}), bf16[1,8,320,2304]{3,2,0,1:T(8,128)(2,1)}, u32[]{:S(2)}, u32[]{:S(2)}) %all-to-all-start) | async-done | bytes 11796512 | tf_op jit(solution)/shard_map/all_to_all | solution.py:54
  190.9 54.3 %all-gather.4.cloned.1.call-done = bf16[1,2304,5760]{2,1,0:T(8,128)(2,1)} async-done(((bf16[1,576,5760]{2,1,0:T(8,128)(2,1)}), bf16[1,2304,5760]{2,1,0:T(8,128)(2,1)}) %all-gather.4.cloned.1.call-update) | async-done | bytes 26542096 | tf_op jit(solution)/shard_map/all_gather | solution.py:55
  245.2 83.5 %fusion.3 = f32[2560,5760]{1,0:T(8,128)} fusion(bf16[2560,2304]{1,0:T(8,128)(2,1)} %bitcast.5, bf16[1,2304,5760]{2,1,0:T(8,128)(2,1)} %all-gather.4.cloned.1.call-done), kind=kOutput, calls=%fused_computation.7 | convolution fusion | flops 67947724800 | bytes 97320960 | tf_op jit(solution)/shard_map/erd,edf->erf/dot_general | solution.py:34
  328.8 152.4 %all-gather.6.cloned.1.call-done = bf16[1,2304,5760]{2,1,0:T(8,128)(2,1)} async-done(((bf16[1,576,5760]{2,1,0:T(8,128)(2,1)}), bf16[1,2304,5760]{2,1,0:T(8,128)(2,1)}) %all-gather.6.cloned.1.call-update) | async-done | bytes 26542096 | tf_op jit(solution)/shard_map/all_gather | solution.py:56
  481.1 92.1 %multiply_convert_fusion = bf16[2560,5760]{1,0:T(8,128)(2,1)} fusion(f32[2560,5760]{1,0:T(8,128)} %fusion.3, bf16[2560,2304]{1,0:T(8,128)(2,1)} %bitcast.5, bf16[1,2304,5760]{2,1,0:T(8,128)(2,1)} %all-gather.6.cloned.1.call-done), kind=kOutput, calls=%fused_computation.3 | convolution fusion | flops 68036198400 | bytes 126812160 | tf_op jit(solution)/shard_map/erd,edf->erf/dot_general | solution.py:35
  573.2 143.8 %all-gather.8.cloned.1.call-done = bf16[1,5760,2304]{1,2,0:T(8,128)(2,1)} async-done(((bf16[1,5760,576]{1,2,0:T(8,128)(2,1)}), bf16[1,5760,2304]{1,2,0:T(8,128)(2,1)}) %all-gather.8.cloned.1.call-update) | async-done | bytes 26542096 | tf_op jit(solution)/shard_map/all_gather | solution.py:57
  717.0 80.1 %fusion.5 = bf16[2560,2304]{1,0:T(8,128)(2,1)} fusion(bf16[2560,5760]{1,0:T(8,128)(2,1)} %multiply_convert_fusion, bf16[1,5760,2304]{1,2,0:T(8,128)(2,1)} %all-gather.8.cloned.1.call-done), kind=kOutput, calls=%fused_computation.11 | convolution fusion | flops 67953623040 | bytes 67829760 | tf_op jit(solution)/shard_map/erf,efd->erd/dot_general | solution.py:37
  797.2 0.0 copy-start.1
  797.2 6.2 all-to-all-start.1
  803.4 0.0 copy-done.3
  803.4 0.5 reduce_sum.23
  803.9 0.0 copy-done.7
  803.9 0.2 copy.18
  804.1 0.0 copy-done.5
  804.2 0.0 copy-done.1
  804.2 0.2 compare_and_fusion
  804.4 126.8 %all-to-all-done.1 = bf16[1,8,320,2304]{3,2,0,1:T(8,128)(2,1)} async-done(((bf16[1,8,320,2304]{3,2,0,1:T(8,128)(2,1)}), bf16[1,8,320,2304]{3,2,0,1:T(8,128)(2,1)}, u32[]{:S(2)}, u32[]{:S(2)}) %all-to-all-start.1) | async-done | bytes 11796512 | tf_op jit(solution)/shard_map/all_to_all | solution.py:59
  931.2 24.1 %gather_fusion.1 = bf16[2048,2304]{1,0:T(8,128)(2,1)} fusion(bf16[2560,2304]{1,0:T(8,128)(2,1)} %bitcast.11, s32[2048]{0:T(1024)S(1)} %broadcast_clamp_fusion), kind=kCustom, calls=%fused_computation.1 | custom fusion | bytes 18882560 | tf_op jit(solution)/shard_map/jit(_take)/gather | solution.py:28
  955.3 19.0 %gather.15 = bf16[1024,2,2304]{2,1,0:T(2,128)(2,1)} reshape(bf16[2048,2304]{1,0:T(8,128)(2,1)} %gather_fusion.1) | data formatting | bytes 18874368 | tf_op jit(solution)/shard_map/jit(_take)/gather | solution.py:28
  974.3 47.6 %multiply_reduce_fusion = f32[1024,2304]{1,0:T(8,128)} fusion(bf16[1024,2,2304]{2,1,0:T(2,128)(2,1)} %gather.15, pred[1024,2]{1,0:T(8,128)(4,1)S(1)} %compare_and_fusion, f32[1024,2]{1,0:T(8,128)S(1)} %copy.18), kind=kLoop, calls=%fused_computation.9 | loop fusion | flops 16515072 | bytes 18884608 | tf_op jit(solution)/shard_map/reduce_sum | solution.py:29
  1021.9 8.2 add_convert_fusion
  (12 shorter events, 0.1 us)
Async XLA Ops:
  6.5 1.6 copy-start.6
  6.5 238.7 %all-gather.4.cloned.1.call-start = ((), (), s32[]{:S(2)}) async-start(), calls=%async_computation.2 | async-start | bytes 33177600 | tf_op jit(solution)/shard_map/all_gather | solution.py:55
  7.3 473.8 %all-gather.6.cloned.1.call-start = ((), (), s32[]{:S(2)}) async-start(), calls=%async_computation.3 | async-start | bytes 33177600 | tf_op jit(solution)/shard_map/all_gather | solution.py:56
  8.4 38.1 %copy-start = (s32[1024,2]{1,0:T(8,128)}, s32[1024,2]{1,0:T(8,128)S(1)}, u32[]{:S(2)}) copy-start(s32[1024,2]{1,0:T(8,128)S(1)} %copy.13) | copy-start | bytes 24580
  12.2 0.6 copy-start.2
  12.8 33.7 %copy-start.4 = (s32[2048,1]{0,1:T(1,128)}, s32[2048,1]{0,1:T(1,128)S(1)}, u32[]{:S(2)}) copy-start(s32[2048,1]{0,1:T(1,128)S(1)} %compare_select_fusion.1) | copy-start | bytes 24580
  56.8 134.0 %all-to-all-start = ((bf16[1,8,320,2304]{3,2,0,1:T(8,128)(2,1)}), bf16[1,8,320,2304]{3,2,0,1:T(8,128)(2,1)}, u32[]{:S(2)}, u32[]{:S(2)}) async-start(bf16[1,8,320,2304]{3,2,0,1:T(8,128)(2,1)} %broadcast_select_fusion.1), calls=%async_computation | async-start | bytes 23592960 | tf_op jit(solution)/shard_map/all_to_all | solution.py:54
  63.0 654.0 %all-gather.8.cloned.1.call-start = ((), (), s32[]{:S(2)}) async-start(), calls=%async_computation.4 | async-start | bytes 33177600 | tf_op jit(solution)/shard_map/all_gather | solution.py:57
  797.2 6.3 copy-start.3
  797.2 6.7 copy-start.7
  797.2 7.0 copy-start.5
  797.2 7.0 copy-start.1
  797.2 134.0 %all-to-all-start.1 = ((bf16[1,8,320,2304]{3,2,0,1:T(8,128)(2,1)}), bf16[1,8,320,2304]{3,2,0,1:T(8,128)(2,1)}, u32[]{:S(2)}, u32[]{:S(2)}) async-start(bf16[1,8,320,2304]{3,2,0,1:T(8,128)(2,1)} %bitcast.44), calls=%async_computation.1 | async-start | bytes 23592960 | tf_op jit(solution)/shard_map/all_to_all | solution.py:59
Sparse Core Ops, SparseCore 0:
  8.9 236.2 all-gather.3
  246.8 234.2 all-gather.5
  482.7 234.2 all-gather.7
where the time goes:
time: 1050 us; the launch traced here: 1040 us
  waiting for transfers between devices  606 us (58%)
  matrix products  256 us (24%)
  local copies, waits for them, and re-layouts  79.4 us (8%)
  other arithmetic  69.1 us (7%)
  between operations  13.6 us (1%)
  starting transfers between devices  12.7 us (1%)
    all_gather x1, waiting for transfers between devices, device_step(): wu_full = lax.all_gather(wu_loc, 'data', axis=1, tiled=True)  152 us
    all_gather x1, waiting for transfers between devices, device_step(): wd_full = lax.all_gather(wd_loc, 'data', axis=2, tiled=True)  144 us
    all_to_all x1, waiting for transfers between devices, device_step(): recv_rows = lax.all_to_all(send_rows, 'expert', 1, 1, tiled=True)  127 us
    all_to_all x1, waiting for transfers between devices, device_step(): lax.all_to_all(out_rows.reshape(n_local, n_group, capacity, d_model), 'ex...  127 us
    dot_general x1, matrix products, expert_ffn(): jnp.einsum('erd,edf->erf', expert_rows, w_up, preferred_element_type=jnp....  92.1 us
    dot_general x1, matrix products, expert_ffn(): jnp.einsum('erd,edf->erf', expert_rows, w_gate, preferred_element_type=jn...  83.5 us
    dot_general x1, matrix products, expert_ffn(): jnp.einsum('erf,efd->erd', hidden, w_down, preferred_element_type=jnp.flo...  80.1 us
    all_gather x1, waiting for transfers between devices, device_step(): wg_full = lax.all_gather(wg_loc, 'data', axis=1, tiled=True)  54.3 us
  transfers between devices with their start and end apart: 5, of which 5 were waited for; matrix products, arithmetic and copies ran while one was open for 22% of the time, Pallas kernels for 0%

commit v1 on v0

v1 whole, which is shorter than its diff:
```python
import functools

import jax
import jax.numpy as jnp
from jax import lax
from jax.experimental import pallas as pl
from jax.experimental.pallas import tpu as pltpu
from jax.sharding import PartitionSpec as P

MESH = pl.DeviceIdType.MESH
F32 = jnp.float32
BF16 = jnp.bfloat16
LEAD = 4
DOWN_STEP = 12


def capacity_rows(tok_rows, top_k, n_exp):
    return max(8, ((5 * top_k * tok_rows) // (4 * n_exp) + 7) // 8 * 8)


def pick(total, options):
    return next(c for c in options if total % c == 0)


def moe_kernel(dims, idx_ref, gate_ref, x_ref, wg_ref, wu_ref, wd_ref, y_ref, xpar_ref, xrows_ref, gu_ref, wdb_ref, back_ref,
               h, keyt, keyt_par, keyc, gate_e,
               s_x, r_x, s_own, r_own, s_par, r_par, l_loc, l_x,
               s_main, s_a, s_b, s_c, r_gu, l_w,
               t_main, t_a, t_b, t_c, r_wd, l_wd, s_ret, r_back, l_back):
    n_x, tok, d_model, d_q, ffn, cap, fc, n_k, n_w, n_j, tile = dims
    rows = 2 * n_x * cap
    wk = ffn // n_w
    xc = d_model // n_j
    p = lax.axis_index("expert")
    q = lax.axis_index("data")
    cx, cc = p // 2, p % 2
    half = q // 2
    inner = q + 1 - 2 * (q % 2)
    outer = 3 - q
    lead = cc == half

    def dev(x, y, c):
        return {"expert": 2 * x + c, "data": y}

    def quarter(i):
        base = q + (i // 2) * (inner - q)
        return base + (i % 2) * (3 - 2 * base)

    partner = dev(cx, q, 1 - cc)
    inner_dev = dev(cx, inner, cc)
    outer_dev = dev(cx, outer, 1 - cc)
    mirror = dev(cx, outer, cc)

    def remote(src, dst, send, recv, device):
        return pltpu.make_async_remote_copy(src_ref=src, dst_ref=dst, send_sem=send, recv_sem=recv, device_id=device, device_id_type=MESH)

    def wait_for(ref, sem):
        pltpu.make_async_copy(ref, ref, sem).wait()

    barrier = pltpu.get_barrier_semaphore()
    peers = [partner, inner_dev, outer_dev]
    peers += [dev((cx + d) % n_x, q, cc) for d in range(1, n_x)]
    peers += [dev((cx + d) % n_x, outer, cc) for d in range(n_x)]
    for peer in peers:
        pl.semaphore_signal(barrier, inc=1, device_id=peer, device_id_type=MESH)
    pl.semaphore_wait(barrier, len(peers))

    def gu_rows(k, i):
        return gu_ref.at[k, pl.ds(quarter(i) * d_q, d_q), :]

    def send_own_gu(k, device, send, recv):
        src = pl.ds(pl.multiple_of(k * fc, 128), fc)
        for w_ref, c0 in ((wg_ref, 0), (wu_ref, fc)):
            remote(w_ref.at[:, src], gu_ref.at[k, pl.ds(q * d_q, d_q), pl.ds(c0, fc)], send, recv, device).start()

    def pass_gu(k, i, device, send, i_there):
        remote(gu_rows(k, i), gu_rows(k, i), send, r_gu.at[i_there, k], device).start()

    for j in range(n_j):
        cols = pl.ds(j * xc, xc)
        remote(x_ref.at[:, cols], xpar_ref.at[:, cols], s_x.at[j], r_x.at[j], mirror).start()

    def start_gu(k, carry):
        @pl.when(lead)
        def _():
            send_own_gu(k, inner_dev, s_main.at[k], r_gu.at[2, k])

        @pl.when(jnp.logical_not(lead))
        def _():
            send_own_gu(k, outer_dev, s_main.at[k], r_gu.at[1, k])

        return carry

    lax.fori_loop(0, n_k, start_gu, 0)

    own_x = pltpu.make_async_copy(x_ref, h.at[pl.ds(0, tok), pl.ds(d_model, d_model)], l_x.at[0])
    own_x.start()
    lane = lax.broadcasted_iota(jnp.int32, (tok, 128), 1)
    first = lane == idx_ref[:, 0:1]
    second = lane == idx_ref[:, 1:2]
    chosen = jnp.logical_or(first, second)
    before = lax.broadcasted_iota(jnp.int32, (tok, tok), 0) > lax.broadcasted_iota(jnp.int32, (tok, tok), 1)
    slot = jnp.dot(before.astype(F32).astype(BF16), chosen.astype(F32).astype(BF16), preferred_element_type=F32)
    key = jnp.where(jnp.logical_and(chosen, slot < cap), slot, -1.0)
    keyc[...] = key
    keyt[...] = key.T[:8, :]
    gate_e[...] = jnp.where(first, gate_ref[:, 0:1], 0.0) + jnp.where(second, gate_ref[:, 1:2], 0.0)
    send_key = remote(keyt, keyt_par, s_x.at[n_j], r_x.at[n_j], mirror)
    send_key.start()

    slots = lax.broadcasted_iota(jnp.int32, (cap, tok), 0).astype(F32)

    def select(keys, d):
        e = 2 * lax.rem(cx + d, n_x) + half
        return (slots == keys[pl.ds(e, 1), :]).astype(F32).astype(BF16)

    own_x.wait()

    def own_rows(t, carry):
        d = lax.rem(t + 1, n_x)
        pick_rows = select(keyt, d)
        stage = h.at[pl.ds(pl.multiple_of(t * cap, 8), cap), pl.ds(0, d_model)]
        for j in range(n_j):
            got = jnp.dot(pick_rows, h[pl.ds(0, tok), pl.ds(d_model + j * xc, xc)], preferred_element_type=F32)
            h[pl.ds(pl.multiple_of(t * cap, 8), cap), pl.ds(j * xc, xc)] = got.astype(BF16)
        dst = xrows_ref.at[pl.ds(pl.multiple_of(cx * 2 * cap, 8), cap), :]

        @pl.when(t < n_x - 1)
        def _():
            remote(stage, dst, s_own.at[t], r_own, dev(lax.rem(cx + d, n_x), q, cc)).start()

        @pl.when(t == n_x - 1)
        def _():
            pltpu.make_async_copy(stage, dst, l_loc.at[n_j]).start()

        return carry

    lax.fori_loop(0, n_x, own_rows, 0)

    def start_own_pass(k, carry):
        @pl.when(lead)
        def _():
            send_own_gu(k, partner, s_a.at[k], r_gu.at[0, k])

        return carry

    lax.fori_loop(0, n_k, start_own_pass, 0)

    send_key.wait()

    def par_cols(j, carry):
        cols = pl.ds(pl.multiple_of(j * xc, 128), xc)
        wait_for(xpar_ref.at[:, cols], r_x.at[j])
        here = pl.ds(pl.multiple_of(d_model + j * xc, 128), xc)
        load = pltpu.make_async_copy(xpar_ref.at[:, cols], h.at[pl.ds(tok, tok), here], l_x.at[1])
        load.start()
        load.wait()

        def par_rows(t, carry2):
            d = lax.rem(t + 1, n_x)
            r0 = pl.multiple_of((n_x + t) * cap, 8)
            got = jnp.dot(select(keyt_par, d), h[pl.ds(tok, tok), here], preferred_element_type=F32)
            h[pl.ds(r0, cap), cols] = got.astype(BF16)
            stage = h.at[pl.ds(r0, cap), cols]
            dst = xrows_ref.at[pl.ds(pl.multiple_of((cx * 2 + 1) * cap, 8), cap), cols]

            @pl.when(t < n_x - 1)
            def _():
                remote(stage, dst, s_par.at[t, j], r_par, dev(lax.rem(cx + d, n_x), q, cc)).start()

            @pl.when(t == n_x - 1)
            def _():
                pltpu.make_async_copy(stage, dst, l_loc.at[j]).start()

            return carry2

        return lax.fori_loop(0, n_x, par_rows, carry)

    lax.fori_loop(0, n_j, par_cols, 0)

    def ahead(k):
        @pl.when(lead)
        def _():
            wait_for(gu_rows(k, 2), r_gu.at[2, k])
            pass_gu(k, 2, partner, s_b.at[k], 2)

        @pl.when(jnp.logical_not(lead))
        def _():
            wait_for(gu_rows(k, 1), r_gu.at[1, k])
            pass_gu(k, 1, inner_dev, s_a.at[k], 3)
            pass_gu(k, 1, partner, s_b.at[k], 1)

    def wd_rows(i, m):
        return wdb_ref.at[quarter(i), pl.ds(pl.multiple_of(m * wk, 8), wk), :]

    def send_own_wd(m, device, send, recv):
        src = wd_ref.at[pl.ds(pl.multiple_of(m * wk, 8), wk), :]
        remote(src, wd_rows(0, m), send, recv, device).start()

    def phase_up(xr, wbuf):
        def gather_chunk(k, slot):
            @pl.when(lead)
            def _():
                wait_for(gu_rows(k, 1), r_gu.at[1, k])
                wait_for(gu_rows(k, 3), r_gu.at[3, k])
                src = pl.ds(pl.multiple_of(k * fc, 128), fc)
                for w_ref, c0 in ((wg_ref, 0), (wu_ref, fc)):
                    pltpu.make_async_copy(w_ref.at[:, src], wbuf.at[slot, pl.ds(q * d_q, d_q), pl.ds(c0, fc)], l_w.at[slot]).start()
                for i in (1, 2, 3):
                    pltpu.make_async_copy(gu_rows(k, i), wbuf.at[slot, pl.ds(quarter(i) * d_q, d_q), :], l_w.at[slot]).start()

            @pl.when(jnp.logical_not(lead))
            def _():
                wait_for(gu_rows(k, 3), r_gu.at[3, k])
                pass_gu(k, 3, partner, s_c.at[k], 3)
                wait_for(gu_rows(k, 0), r_gu.at[0, k])
                wait_for(gu_rows(k, 2), r_gu.at[2, k])
                pltpu.make_async_copy(gu_ref.at[k], wbuf.at[slot], l_w.at[slot]).start()

        for k in range(LEAD):
            ahead(k)

        wait_for(xrows_ref.at[pl.ds(0, (n_x - 1) * cap), :], r_own)
        wait_for(xrows_ref.at[pl.ds(0, (n_x - 1) * cap), :], r_par)
        wait_for(xrows_ref.at[pl.ds(0, cap), :], l_loc.at[n_j])
        for j in range(n_j):
            wait_for(xrows_ref.at[pl.ds(0, cap), pl.ds(0, xc)], l_loc.at[j])
        load = pltpu.make_async_copy(xrows_ref, xr, l_x.at[0])
        load.start()

        def drain(t, carry):
            wait_for(xrows_ref.at[pl.ds(0, cap), :], s_own.at[t])

            def inner_drain(j, carry2):
                wait_for(xrows_ref.at[pl.ds(0, cap), pl.ds(0, xc)], s_par.at[t, j])
                return carry2

            return lax.fori_loop(0, n_j, inner_drain, carry)

        lax.fori_loop(0, n_x - 1, drain, 0)
        for j in range(n_j):
            wait_for(xpar_ref.at[:, pl.ds(0, xc)], s_x.at[j])

        def start_wd(m, carry):
            @pl.when(jnp.logical_not(lead))
            def _():
                send_own_wd(m, outer_dev, t_main.at[m], r_wd.at[1, m])

            @pl.when(lead)
            def _():
                send_own_wd(m, partner, t_a.at[m], r_wd.at[0, m])

            return carry

        lax.fori_loop(0, n_w, start_wd, 0)
        gather_chunk(0, 0)
        load.wait()

        def step(k, carry):
            slot = lax.rem(k, 2)

            @pl.when(k + LEAD < n_k)
            def _():
                ahead(k + LEAD)

            @pl.when(jnp.logical_and(k == min(DOWN_STEP, n_k - 1), lead))
            def _():
                def start_near(m, carry2):
                    send_own_wd(m, inner_dev, t_main.at[m], r_wd.at[2, m])
                    return carry2

                lax.fori_loop(0, n_w, start_near, 0)

            @pl.when(k + 1 < n_k)
            def _():
                gather_chunk(k + 1, lax.rem(k + 1, 2))

            wait_for(wbuf.at[slot], l_w.at[slot])

            def row_tile(r, carry2):
                r0 = pl.multiple_of(r * tile, 8)
                both = jnp.dot(xr[pl.ds(r0, tile), :], wbuf[slot], preferred_element_type=F32)
                act = jax.nn.silu(both[:, :fc]) * both[:, fc:]
                h[pl.ds(r0, tile), pl.ds(pl.multiple_of(k * fc, 128), fc)] = act.astype(BF16)
                return carry2

            lax.fori_loop(0, rows // tile, row_tile, 0)
            return carry

        lax.fori_loop(0, n_k, step, 0)

    def phase_down(wdv, stage, acc, cmat, backv):
        t_tile = min(256, tok)

        def ret_dst(i):
            return back_ref.at[quarter(i), half, pl.ds(pl.multiple_of(cx * cap, 8), cap), :]

        def load_wd(i):
            def load_part(m, carry):
                dst = wdv.at[pl.ds(pl.multiple_of(m * wk, 8), wk), :]

                @pl.when(jnp.logical_and(lead, i == 0))
                def _():
                    pltpu.make_async_copy(wd_ref.at[pl.ds(pl.multiple_of(m * wk, 8), wk), :], dst, l_wd.at[m]).start()

                @pl.when(jnp.logical_not(jnp.logical_and(lead, i == 0)))
                def _():
                    wait_for(wd_rows(i, m), r_wd.at[i, m])

                    @pl.when(jnp.logical_and(lead, i == 2))
                    def _():
                        remote(wd_rows(2, m), wd_rows(2, m), t_b.at[m], r_wd.at[2, m], partner).start()

                    @pl.when(jnp.logical_and(jnp.logical_not(lead), i == 1))
                    def _():
                        remote(wd_rows(1, m), wd_rows(1, m), t_b.at[m], r_wd.at[1, m], partner).start()

                    @pl.when(jnp.logical_and(jnp.logical_not(lead), i == 3))
                    def _():
                        remote(wd_rows(3, m), wd_rows(3, m), t_c.at[m], r_wd.at[3, m], partner).start()

                    pltpu.make_async_copy(wd_rows(i, m), dst, l_wd.at[m]).start()

                return carry

            lax.fori_loop(0, n_w, load_part, 0)
            for m in range(n_w):
                wait_for(wdv.at[pl.ds(m * wk, wk), :], l_wd.at[m])

        def combine(qt, g, add):
            load = pltpu.make_async_copy(back_ref.at[qt, g], backv, l_back)
            load.start()
            load.wait()

            def tok_tile(r, carry):
                r0 = pl.multiple_of(r * t_tile, 8)
                gates = gate_e[pl.ds(r0, t_tile), :]
                lanes = lax.broadcasted_iota(jnp.int32, (t_tile, 128), 1)
                total = None
                for x in range(n_x):
                    e = 2 * x + g
                    rows_x = jnp.dot(cmat[e, pl.ds(r0, t_tile), :], backv[pl.ds(x * cap, cap), :], preferred_element_type=F32)
                    gate_x = jnp.sum(jnp.where(lanes == e, gates, 0.0), axis=1, keepdims=True)
                    total = gate_x * rows_x if total is None else total + gate_x * rows_x
                if add:
                    total = total + acc[qt, pl.ds(r0, t_tile), :]
                acc[qt, pl.ds(r0, t_tile), :] = total
                return carry

            lax.fori_loop(0, tok // t_tile, tok_tile, 0)

        def units(i):
            def both(add):
                wait_for(back_ref.at[0, 0, pl.ds(0, (n_x - 1) * cap), :], r_back.at[quarter(i), half])
                combine(quarter(i), half, add)
                wait_for(back_ref.at[0, 0], r_back.at[3 - quarter(i), 1 - half])
                combine(3 - quarter(i), 1 - half, add)

            @pl.when(i % 2 == 0)
            def _():
                both(False)

            @pl.when(i % 2 == 1)
            def _():
                both(True)

        def piece(i, carry):
            load_wd(i)

            def block(t, carry2):
                s = 1 - t // n_x
                x_src = lax.rem(cx + 1 + t % n_x, n_x)
                r0 = pl.multiple_of((x_src * 2 + s) * cap, 8)
                out = jnp.dot(h[pl.ds(r0, cap), :], wdv[...], preferred_element_type=F32)

                @pl.when(i > 0)
                def _():
                    wait_for(stage.at[t], s_ret.at[t])

                stage[t] = out.astype(BF16)

                @pl.when(t < 2 * n_x - 1)
                def _():
                    remote(stage.at[t], ret_dst(i), s_ret.at[t], r_back.at[quarter(i), half], dev(x_src, q + s * (outer - q), cc)).start()

                @pl.when(t == 2 * n_x - 1)
                def _():
                    pltpu.make_async_copy(stage.at[t], ret_dst(i), s_ret.at[t]).start()

                return carry2

            lax.fori_loop(0, 2 * n_x, block, 0)

            @pl.when(jnp.logical_and(i == 1, jnp.logical_not(lead)))
            def _():
                def near(m, carry2):
                    remote(wd_rows(1, m), wd_rows(1, m), t_a.at[m], r_wd.at[3, m], inner_dev).start()
                    return carry2

                lax.fori_loop(0, n_w, near, 0)

            @pl.when(i == 0)
            def _():
                slot_lane = lax.broadcasted_iota(jnp.int32, (tok, cap), 1).astype(F32)
                for e in range(2 * n_x):
                    cmat[e] = (slot_lane == keyc[:, e:e + 1]).astype(F32).astype(BF16)

            @pl.when(i > 0)
            def _():
                units(i - 1)

            return carry

        lax.fori_loop(0, 4, piece, 0)

        x_here = h.at[pl.ds(0, tok), pl.ds(0, d_model)]
        load = pltpu.make_async_copy(x_ref, x_here, l_x.at[0])
        load.start()
        for t in range(2 * n_x):
            wait_for(stage.at[t], s_ret.at[t])
        units(jnp.int32(3))
        load.wait()

        def finish(r, carry):
            r0 = pl.multiple_of(r * t_tile, 8)
            for qt in range(4):
                cols = pl.ds(qt * d_q, d_q)
                total = h[pl.ds(r0, t_tile), cols].astype(F32) + acc[qt, pl.ds(r0, t_tile), :]
                h[pl.ds(r0, t_tile), cols] = total.astype(BF16)
            return carry

        lax.fori_loop(0, tok // t_tile, finish, 0)
        store = pltpu.make_async_copy(x_here, y_ref, l_x.at[0])
        store.start()
        store.wait()

    pl.run_scoped(phase_up, pltpu.VMEM((rows, d_model), BF16), pltpu.VMEM((2, d_model, 2 * fc), BF16))
    pl.run_scoped(
        phase_down,
        pltpu.VMEM((ffn, d_q), BF16),
        pltpu.VMEM((2 * n_x, cap, d_q), BF16),
        pltpu.VMEM((4, tok, d_q), F32),
        pltpu.VMEM((2 * n_x, tok, cap), BF16),
        pltpu.VMEM((n_x * cap, d_q), BF16),
    )

    def drain_gu(k, carry):
        wait_for(gu_rows(k, 0), s_main.at[k])
        wait_for(gu_rows(k, 0), s_a.at[k])
        wait_for(gu_rows(k, 0), s_b.at[k])

        @pl.when(jnp.logical_not(lead))
        def _():
            wait_for(gu_rows(k, 0), s_c.at[k])

        return carry

    lax.fori_loop(0, n_k, drain_gu, 0)

    def drain_wd(m, carry):
        wait_for(wd_rows(0, m), t_main.at[m])
        wait_for(wd_rows(0, m), t_a.at[m])
        wait_for(wd_rows(0, m), t_b.at[m])

        @pl.when(jnp.logical_not(lead))
        def _():
            wait_for(wd_rows(0, m), t_c.at[m])

        return carry

    lax.fori_loop(0, n_w, drain_wd, 0)


def solution(mesh):
    n_group, n_y = mesh.shape["expert"], mesh.shape["data"]
    assert n_y == 4 and n_group % 2 == 0
    n_x = n_group // 2
    tok_spec = P(("rep", "expert", "data"), None)
    wide_spec = P("expert", "data", None)
    down_spec = P("expert", None, "data")

    def device_step(x_loc, idx_loc, gate_loc, wg_loc, wu_loc, wd_loc):
        tok, d_model = x_loc.shape
        n_local, d_q, ffn = wg_loc.shape
        assert n_local == 1 and n_group == 8
        cap = capacity_rows(tok, idx_loc.shape[1], n_group)
        fc = pick(ffn, (384, 256, 128))
        n_k, n_w, n_j = ffn // fc, pick(ffn // 16, (3, 2, 1)), pick(d_model // 128, (3, 2, 1))
        rows = 2 * n_x * cap
        tile = pick(rows, (640, 48, 8))
        dims = (n_x, tok, d_model, d_q, ffn, cap, fc, n_k, n_w, n_j, tile)
        hbm = pl.BlockSpec(memory_space=pl.ANY)
        vmem = pl.BlockSpec(memory_space=pltpu.VMEM)
        dma = pltpu.SemaphoreType.DMA
        shape = jax.ShapeDtypeStruct
        outs = pl.pallas_call(
            functools.partial(moe_kernel, dims),
            name="moe_layer",
            out_shape=[
                shape((tok, d_model), BF16),
                shape((tok, d_model), BF16),
                shape((rows, d_model), BF16),
                shape((n_k, d_model, 2 * fc), BF16),
                shape((4, ffn, d_q), BF16),
                shape((4, 2, n_x * cap, d_q), BF16),
            ],
            in_specs=[vmem, vmem, hbm, hbm, hbm, hbm],
            out_specs=[hbm] * 6,
            scratch_shapes=[
                pltpu.VMEM((rows, ffn), BF16),
                pltpu.VMEM((8, tok), F32),
                pltpu.VMEM((8, tok), F32),
                pltpu.VMEM((tok, 128), F32),
                pltpu.VMEM((tok, 128), F32),
                dma((n_j + 1,)), dma((n_j + 1,)), dma((n_x - 1,)), dma, dma((n_x - 1, n_j)), dma, dma((n_j + 1,)), dma((2,)),
                dma((n_k,)), dma((n_k,)), dma((n_k,)), dma((n_k,)), dma((4, n_k)), dma((2,)),
                dma((n_w,)), dma((n_w,)), dma((n_w,)), dma((n_w,)), dma((4, n_w)), dma((n_w,)),
                dma((2 * n_x,)), dma((4, 2)), dma,
            ],
            compiler_params=pltpu.CompilerParams(collective_id=0, has_side_effects=True, vmem_limit_bytes=67_043_328),
        )(idx_loc, gate_loc, x_loc, wg_loc.reshape(d_q, ffn), wu_loc.reshape(d_q, ffn), wd_loc.reshape(ffn, d_q))
        return outs[0]

    return jax.shard_map(device_step, mesh=mesh, in_specs=(tok_spec, tok_spec, tok_spec, wide_spec, wide_spec, down_spec), out_specs=tok_spec, check_vma=False)
```

time: 1050 us -> 704 us (0.67); the launches traced: 1040 us -> 702 us
  Pallas kernels: 0 us -> 683 us
  waiting for transfers between devices: 606 us -> 0 us
  matrix products: 256 us -> 0 us
  other arithmetic: 69.1 us -> 0 us
  local copies, waits for them, and re-layouts: 79.4 us -> 18.5 us
  between operations: 13.6 us -> 0.01 us
  starting transfers between devices: 12.7 us -> 0 us
    pallas_call x0 -> x1, Pallas kernels: none -> 683 us  [device_step(): pl.pallas_call(functools.partial(moe_kernel, dims), name='moe_layer', out...]
    all_gather x3 -> x0, waiting for transfers between devices: 350 us -> none  [the longest x1 152 us: device_step(): wu_full = lax.all_gather(wu_loc, 'data', axis=1, tiled=True)]
    dot_general x3 -> x0, matrix products: 256 us -> none  [the longest x1 92.1 us: expert_ffn(): jnp.einsum('erd,edf->erf', expert_rows, w_up, preferred_element_type=jnp....]
    all_to_all x2 -> x0, waiting for transfers between devices: 254 us -> none  [the longest x1 127 us: device_step(): recv_rows = lax.all_to_all(send_rows, 'expert', 1, 1, tiled=True)]
    gather x3 -> x0, local copies, waits for them, and re-layouts: 68.6 us -> none  [the longest x2 43.1 us: combine_rows(): pair_out = jnp.take(back_rows, dest_row, axis=0, mode='fill', fill_value=0)]
    reduce_sum x2 -> x0, other arithmetic: 47.7 us -> none  [the longest x1 47.6 us: combine_rows(): jnp.sum(pair_out.reshape(tok_rows, gate_loc.shape[1], d_model) * gate_loc...]
    unnamed x18 -> x4, local copies, waits for them, and re-layouts: 1.04 us -> 18.5 us
    all_to_all x2 -> x0, starting transfers between devices: 12.3 us -> none  [the longest x1 6.22 us: device_step(): lax.all_to_all(out_rows.reshape(n_local, n_group, capacity, d_model), 'ex...]
  transfers between devices with their start and end apart: 5 -> 0, of which waited for: 5 -> 0; matrix products, arithmetic and copies ran while one was open for 22% -> 0% of each run, Pallas kernels for 0% -> 0%
where the time goes in v1:
time: 704 us; the launch traced here: 702 us
  Pallas kernels  683 us (97%)
  local copies, waits for them, and re-layouts  18.5 us (3%)
    pallas_call x1, Pallas kernels, device_step(): pl.pallas_call(functools.partial(moe_kernel, dims), name='moe_layer', out...  683 us
    unnamed x4, local copies, waits for them, and re-layouts  18.5 us

profile of v1, /device:TPU:100, one launch (start us, length us, event | category | flops | bytes accessed | tf_op | source)
XLA Modules:
  0.0 701.6 jit_solution(6317965957714044258)
XLA Ops:
  0.0 1.7 copy.8.idx_ref
  1.7 1.7 copy.9.gate_ref
  3.4 10.3 %copy.7 = bf16[1,5760,576]{2,1,0:T(8,128)(2,1)} copy(bf16[1,5760,576]{1,2,0:T(8,128)(2,1)} %param.11) | data formatting | bytes 13271040 | tf_op args[5]
  13.7 683.1 %moe_layer.1 = (bf16[1024,2304]{1,0:T(8,128)(2,1)}, bf16[1024,2304]{1,0:T(8,128)(2,1)}, bf16[2560,2304]{1,0:T(8,128)(2,1)}, bf16[15,2304,768]{2,1,0:T(8,128)(2,1...) custom-call(s32[1024,2]{1,0:T(8,128)} %copy.8.idx_ref, f32[1024,2]{1,0:T(8,128)} %copy.9.gate_ref, ...), custom_call_target="tpu_custom_call" | custom-call | tf_op jit(solution)/shard_map/moe_layer/pallas_call | solution.py:496
  696.8 4.8 copy.11

commit v2 on v1

--- a/solution.py
+++ b/solution.py
@@ -11,7 +11,9 @@
 F32 = jnp.float32
 BF16 = jnp.bfloat16
 LEAD = 4
+EARLY = 11
 DOWN_STEP = 12
+LAG = 3
 
 
 def capacity_rows(tok_rows, top_k, n_exp):
@@ -29,7 +31,7 @@
                t_main, t_a, t_b, t_c, r_wd, l_wd, s_ret, r_back, l_back):
     n_x, tok, d_model, d_q, ffn, cap, fc, n_k, n_w, n_j, tile = dims
     rows = 2 * n_x * cap
-    wk = ffn // n_w
+    wk = d_q // n_w
     xc = d_model // n_j
     p = lax.axis_index("expert")
     q = lax.axis_index("data")
@@ -76,37 +78,41 @@
     def pass_gu(k, i, device, send, i_there):
         remote(gu_rows(k, i), gu_rows(k, i), send, r_gu.at[i_there, k], device).start()
 
-    for j in range(n_j):
+    def send_block(j):
         cols = pl.ds(j * xc, xc)
         remote(x_ref.at[:, cols], xpar_ref.at[:, cols], s_x.at[j], r_x.at[j], mirror).start()
 
-    def start_gu(k, carry):
-        @pl.when(lead)
-        def _():
-            send_own_gu(k, inner_dev, s_main.at[k], r_gu.at[2, k])
-
-        @pl.when(jnp.logical_not(lead))
-        def _():
-            send_own_gu(k, outer_dev, s_main.at[k], r_gu.at[1, k])
-
-        return carry
-
-    lax.fori_loop(0, n_k, start_gu, 0)
+    def each(count, body):
+        lax.fori_loop(0, count, lambda k, carry: (body(k), carry)[1], 0)
+
+    send_block(0)
+    early = min(EARLY, n_k)
+
+    @pl.when(lead)
+    def _():
+        each(early, lambda k: send_own_gu(k, inner_dev, s_main.at[k], r_gu.at[2, k]))
 
     own_x = pltpu.make_async_copy(x_ref, h.at[pl.ds(0, tok), pl.ds(d_model, d_model)], l_x.at[0])
     own_x.start()
-    lane = lax.broadcasted_iota(jnp.int32, (tok, 128), 1)
-    first = lane == idx_ref[:, 0:1]
-    second = lane == idx_ref[:, 1:2]
+    expert = lax.broadcasted_iota(jnp.int32, (128, tok), 0)
+    first = expert == idx_ref[0:1, :]
+    second = expert == idx_ref[1:2, :]
     chosen = jnp.logical_or(first, second)
-    before = lax.broadcasted_iota(jnp.int32, (tok, tok), 0) > lax.broadcasted_iota(jnp.int32, (tok, tok), 1)
-    slot = jnp.dot(before.astype(F32).astype(BF16), chosen.astype(F32).astype(BF16), preferred_element_type=F32)
+    before = lax.broadcasted_iota(jnp.int32, (tok, tok), 0) < lax.broadcasted_iota(jnp.int32, (tok, tok), 1)
+    slot = jnp.dot(chosen.astype(F32).astype(BF16), before.astype(F32).astype(BF16), preferred_element_type=F32)
     key = jnp.where(jnp.logical_and(chosen, slot < cap), slot, -1.0)
-    keyc[...] = key
-    keyt[...] = key.T[:8, :]
-    gate_e[...] = jnp.where(first, gate_ref[:, 0:1], 0.0) + jnp.where(second, gate_ref[:, 1:2], 0.0)
+    keyt[...] = key[:8, :]
+    keyc[...] = key.T
+    gate_e[...] = (jnp.where(first, gate_ref[0:1, :], 0.0) + jnp.where(second, gate_ref[1:2, :], 0.0)).T
     send_key = remote(keyt, keyt_par, s_x.at[n_j], r_x.at[n_j], mirror)
     send_key.start()
+    for j in range(1, n_j):
+        send_block(j)
+
+    @pl.when(jnp.logical_not(lead))
+    def _():
+        each(n_k, lambda k: send_own_gu(k, outer_dev, s_main.at[k], r_gu.at[1, k]))
+
 
     slots = lax.broadcasted_iota(jnp.int32, (cap, tok), 0).astype(F32)
 
@@ -263,6 +269,10 @@
             def _():
                 ahead(k + LEAD)
 
+            @pl.when(jnp.logical_and(lead, jnp.logical_and(k >= 2, k - 2 + early < n_k)))
+            def _():
+                send_own_gu(k - 2 + early, inner_dev, s_main.at[k - 2 + early], r_gu.at[2, k - 2 + early])
+
             @pl.when(jnp.logical_and(k == min(DOWN_STEP, n_k - 1), lead))
             def _():
                 def start_near(m, carry2):
@@ -290,48 +300,44 @@
         lax.fori_loop(0, n_k, step, 0)
 
     def phase_down(wdv, stage, acc, cmat, backv):
-        t_tile = min(256, tok)
-
-        def ret_dst(i):
-            return back_ref.at[quarter(i), half, pl.ds(pl.multiple_of(cx * cap, 8), cap), :]
-
-        def load_wd(i):
-            def load_part(m, carry):
-                dst = wdv.at[pl.ds(pl.multiple_of(m * wk, 8), wk), :]
-
-                @pl.when(jnp.logical_and(lead, i == 0))
-                def _():
-                    pltpu.make_async_copy(wd_ref.at[pl.ds(pl.multiple_of(m * wk, 8), wk), :], dst, l_wd.at[m]).start()
-
-                @pl.when(jnp.logical_not(jnp.logical_and(lead, i == 0)))
-                def _():
-                    wait_for(wd_rows(i, m), r_wd.at[i, m])
-
-                    @pl.when(jnp.logical_and(lead, i == 2))
-                    def _():
-                        remote(wd_rows(2, m), wd_rows(2, m), t_b.at[m], r_wd.at[2, m], partner).start()
-
-                    @pl.when(jnp.logical_and(jnp.logical_not(lead), i == 1))
-                    def _():
-                        remote(wd_rows(1, m), wd_rows(1, m), t_b.at[m], r_wd.at[1, m], partner).start()
-
-                    @pl.when(jnp.logical_and(jnp.logical_not(lead), i == 3))
-                    def _():
-                        remote(wd_rows(3, m), wd_rows(3, m), t_c.at[m], r_wd.at[3, m], partner).start()
-
-                    pltpu.make_async_copy(wd_rows(i, m), dst, l_wd.at[m]).start()
-
-                return carry
-
-            lax.fori_loop(0, n_w, load_part, 0)
-            for m in range(n_w):
-                wait_for(wdv.at[pl.ds(m * wk, wk), :], l_wd.at[m])
-
-        def combine(qt, g, add):
-            load = pltpu.make_async_copy(back_ref.at[qt, g], backv, l_back)
-            load.start()
-            load.wait()
-
+        t_tile = min(512, tok)
+        parts = 4 * n_w
+        n_blocks = 2 * n_x
+
+        def ret_dst(u):
+            return back_ref.at[quarter(u // n_w), u % n_w, half, pl.ds(pl.multiple_of(cx * cap, 8), cap), :]
+
+        def take(i, m):
+            @pl.when(jnp.logical_not(jnp.logical_and(lead, i == 0)))
+            def _():
+                wait_for(wd_rows(i, m), r_wd.at[i, m])
+
+                @pl.when(jnp.logical_and(lead, i == 2))
+                def _():
+                    remote(wd_rows(2, m), wd_rows(2, m), t_b.at[m], r_wd.at[2, m], partner).start()
+
+                @pl.when(jnp.logical_and(jnp.logical_not(lead), i == 1))
+                def _():
+                    remote(wd_rows(1, m), wd_rows(1, m), t_b.at[m], r_wd.at[1, m], partner).start()
+
+                @pl.when(jnp.logical_and(jnp.logical_not(lead), i == 3))
+                def _():
+                    remote(wd_rows(3, m), wd_rows(3, m), t_c.at[m], r_wd.at[3, m], partner).start()
+
+        def load_part(u):
+            i, m = u // n_w, u % n_w
+            dst = wdv.at[lax.rem(u, 2)]
+            sem = l_wd.at[lax.rem(u, 2)]
+
+            @pl.when(jnp.logical_and(lead, i == 0))
+            def _():
+                pltpu.make_async_copy(wd_ref.at[pl.ds(pl.multiple_of(m * wk, 8), wk), :], dst, sem).start()
+
+            @pl.when(jnp.logical_not(jnp.logical_and(lead, i == 0)))
+            def _():
+                pltpu.make_async_copy(wd_rows(i, m), dst, sem).start()
+
+        def combine(qt, m, g, add, buf):
             def tok_tile(r, carry):
                 r0 = pl.multiple_of(r * t_tile, 8)
                 gates = gate_e[pl.ds(r0, t_tile), :]
@@ -339,22 +345,31 @@
                 total = None
                 for x in range(n_x):
                     e = 2 * x + g
-                    rows_x = jnp.dot(cmat[e, pl.ds(r0, t_tile), :], backv[pl.ds(x * cap, cap), :], preferred_element_type=F32)
+                    rows_x = jnp.dot(cmat[e, pl.ds(r0, t_tile), :], backv[buf, pl.ds(x * cap, cap), :], preferred_element_type=F32)
                     gate_x = jnp.sum(jnp.where(lanes == e, gates, 0.0), axis=1, keepdims=True)
                     total = gate_x * rows_x if total is None else total + gate_x * rows_x
                 if add:
-                    total = total + acc[qt, pl.ds(r0, t_tile), :]
-                acc[qt, pl.ds(r0, t_tile), :] = total
+                    total = total + acc[qt * n_w + m, pl.ds(r0, t_tile), :]
+                acc[qt * n_w + m, pl.ds(r0, t_tile), :] = total
                 return carry
 
             lax.fori_loop(0, tok // t_tile, tok_tile, 0)
 
-        def units(i):
+        def add_up(u):
+            i, m = u // n_w, u % n_w
+            here, there = quarter(i), 3 - quarter(i)
+            wait_for(back_ref.at[0, 0, 0, pl.ds(0, (n_x - 1) * cap), :], r_back.at[here, m, half])
+            first_load = pltpu.make_async_copy(back_ref.at[here, m, half], backv.at[0], l_back.at[0])
+            first_load.start()
+            wait_for(back_ref.at[0, 0, 0], r_back.at[there, m, 1 - half])
+            second_load = pltpu.make_async_copy(back_ref.at[there, m, 1 - half], backv.at[1], l_back.at[1])
+            second_load.start()
+
             def both(add):
-                wait_for(back_ref.at[0, 0, pl.ds(0, (n_x - 1) * cap), :], r_back.at[quarter(i), half])
-                combine(quarter(i), half, add)
-                wait_for(back_ref.at[0, 0], r_back.at[3 - quarter(i), 1 - half])
-                combine(3 - quarter(i), 1 - half, add)
+                first_load.wait()
+                combine(here, m, half, add, 0)
+                second_load.wait()
+                combine(there, m, 1 - half, add, 1)
 
             @pl.when(i % 2 == 0)
             def _():
@@ -364,68 +379,99 @@
             def _():
                 both(True)
 
-        def piece(i, carry):
-            load_wd(i)
+        take(jnp.int32(0), jnp.int32(0))
+        load_part(jnp.int32(0))
+
+        slot_lane = lax.broadcasted_iota(jnp.int32, (tok, cap), 1).astype(F32)
+        for e in range(2 * n_x):
+            cmat[e] = (slot_lane == keyc[:, e:e + 1]).astype(F32).astype(BF16)
+
+        def part(u, carry):
+            i, m = u // n_w, u % n_w
+            slot = lax.rem(u, LAG)
+
+            @pl.when(u >= 2 * n_w)
+            def _():
+                take(i, m)
+                load_part(u)
+
+            @pl.when(u == 1)
+            def _():
+                each(n_w - 2, lambda k: take(jnp.int32(0), k + 2))
+
+                @pl.when(jnp.logical_not(lead))
+                def _():
+                    each(n_w, lambda k: take(jnp.int32(1), k))
+
+            @pl.when(jnp.logical_and(u == n_w - 1, lead))
+            def _():
+                each(n_w, lambda k: take(jnp.int32(1), k))
+
+            @pl.when(jnp.logical_and(u == n_w + 1, jnp.logical_not(lead)))
+            def _():
+                each(n_w, lambda k: remote(wd_rows(1, k), wd_rows(1, k), t_a.at[k], r_wd.at[3, k], inner_dev).start())
+
+            @pl.when(jnp.logical_and(u >= 1, u + 1 < 2 * n_w))
+            def _():
+                load_part(u + 1)
+
+            wait_for(wdv.at[0], l_wd.at[lax.rem(u, 2)])
 
             def block(t, carry2):
-                s = 1 - t // n_x
+                s = (t // n_x + 1 - cc) % 2
                 x_src = lax.rem(cx + 1 + t % n_x, n_x)
                 r0 = pl.multiple_of((x_src * 2 + s) * cap, 8)
-                out = jnp.dot(h[pl.ds(r0, cap), :], wdv[...], preferred_element_type=F32)
-
-                @pl.when(i > 0)
-                def _():
-                    wait_for(stage.at[t], s_ret.at[t])
-
-                stage[t] = out.astype(BF16)
-
-                @pl.when(t < 2 * n_x - 1)
-                def _():
-                    remote(stage.at[t], ret_dst(i), s_ret.at[t], r_back.at[quarter(i), half], dev(x_src, q + s * (outer - q), cc)).start()
-
-                @pl.when(t == 2 * n_x - 1)
-                def _():
-                    pltpu.make_async_copy(stage.at[t], ret_dst(i), s_ret.at[t]).start()
+                out = lax.dot_general(h[pl.ds(r0, cap), :], wdv[lax.rem(u, 2)], (((1,), (1,)), ((), ())), preferred_element_type=F32)
+
+                @pl.when(u >= LAG)
+                def _():
+                    wait_for(stage.at[0, 0], s_ret.at[slot, t])
+
+                stage[slot, t] = out.astype(BF16)
+                local = jnp.logical_and(s == 0, t % n_x == n_x - 1)
+
+                @pl.when(jnp.logical_not(local))
+                def _():
+                    remote(stage.at[slot, t], ret_dst(u), s_ret.at[slot, t], r_back.at[quarter(i), m, half], dev(x_src, q + s * (outer - q), cc)).start()
+
+                @pl.when(local)
+                def _():
+                    pltpu.make_async_copy(stage.at[slot, t], ret_dst(u), s_ret.at[slot, t]).start()
 
                 return carry2
 
-            lax.fori_loop(0, 2 * n_x, block, 0)
-
-            @pl.when(jnp.logical_and(i == 1, jnp.logical_not(lead)))
-            def _():
-                def near(m, carry2):
-                    remote(wd_rows(1, m), wd_rows(1, m), t_a.at[m], r_wd.at[3, m], inner_dev).start()
-                    return carry2
-
-                lax.fori_loop(0, n_w, near, 0)
-
-            @pl.when(i == 0)
-            def _():
-                slot_lane = lax.broadcasted_iota(jnp.int32, (tok, cap), 1).astype(F32)
-                for e in range(2 * n_x):
-                    cmat[e] = (slot_lane == keyc[:, e:e + 1]).astype(F32).astype(BF16)
-
-            @pl.when(i > 0)
-            def _():
-                units(i - 1)
+            lax.fori_loop(0, n_blocks, block, 0)
+
+            @pl.when(u == 0)
+            def _():
+                take(0, jnp.int32(1))
+                load_part(jnp.int32(1))
+
+            @pl.when(u >= LAG)
+            def _():
+                add_up(u - LAG)
 
             return carry
 
-        lax.fori_loop(0, 4, piece, 0)
+        lax.fori_loop(0, parts, part, 0)
 
         x_here = h.at[pl.ds(0, tok), pl.ds(0, d_model)]
         load = pltpu.make_async_copy(x_ref, x_here, l_x.at[0])
         load.start()
-        for t in range(2 * n_x):
-            wait_for(stage.at[t], s_ret.at[t])
-        units(jnp.int32(3))
+
+        def rest(k):
+            u = parts - LAG + k
+            each(n_blocks, lambda t: wait_for(stage.at[0, 0], s_ret.at[lax.rem(u, LAG), t]))
+            add_up(u)
+
+        each(LAG, rest)
         load.wait()
 
         def finish(r, carry):
             r0 = pl.multiple_of(r * t_tile, 8)
-            for qt in range(4):
-                cols = pl.ds(qt * d_q, d_q)
-                total = h[pl.ds(r0, t_tile), cols].astype(F32) + acc[qt, pl.ds(r0, t_tile), :]
+            for c in range(4 * n_w):
+                cols = pl.ds(c * wk, wk)
+                total = h[pl.ds(r0, t_tile), cols].astype(F32) + acc[c, pl.ds(r0, t_tile), :]
                 h[pl.ds(r0, t_tile), cols] = total.astype(BF16)
             return carry
 
@@ -437,11 +483,11 @@
     pl.run_scoped(phase_up, pltpu.VMEM((rows, d_model), BF16), pltpu.VMEM((2, d_model, 2 * fc), BF16))
     pl.run_scoped(
         phase_down,
-        pltpu.VMEM((ffn, d_q), BF16),
-        pltpu.VMEM((2 * n_x, cap, d_q), BF16),
-        pltpu.VMEM((4, tok, d_q), F32),
+        pltpu.VMEM((2, wk, ffn), BF16),
+        pltpu.VMEM((LAG, 2 * n_x, cap, wk), BF16),
+        pltpu.VMEM((4 * n_w, tok, wk), F32),
         pltpu.VMEM((2 * n_x, tok, cap), BF16),
-        pltpu.VMEM((n_x * cap, d_q), BF16),
+        pltpu.VMEM((2, n_x * cap, wk), BF16),
     )
 
     def drain_gu(k, carry):
@@ -485,7 +531,7 @@
         assert n_local == 1 and n_group == 8
         cap = capacity_rows(tok, idx_loc.shape[1], n_group)
         fc = pick(ffn, (384, 256, 128))
-        n_k, n_w, n_j = ffn // fc, pick(ffn // 16, (3, 2, 1)), pick(d_model // 128, (3, 2, 1))
+        n_k, n_w, n_j = ffn // fc, pick(d_q // 8, (3, 2, 1)), pick(d_model // 128, (3, 2, 1))
         rows = 2 * n_x * cap
         tile = pick(rows, (640, 48, 8))
         dims = (n_x, tok, d_model, d_q, ffn, cap, fc, n_k, n_w, n_j, tile)
@@ -501,8 +547,8 @@
                 shape((tok, d_model), BF16),
                 shape((rows, d_model), BF16),
                 shape((n_k, d_model, 2 * fc), BF16),
-                shape((4, ffn, d_q), BF16),
-                shape((4, 2, n_x * cap, d_q), BF16),
+                shape((4, d_q, ffn), BF16),
+                shape((4, n_w, 2, n_x * cap, d_q // n_w), BF16),
             ],
             in_specs=[vmem, vmem, hbm, hbm, hbm, hbm],
             out_specs=[hbm] * 6,
@@ -514,11 +560,11 @@
                 pltpu.VMEM((tok, 128), F32),
                 dma((n_j + 1,)), dma((n_j + 1,)), dma((n_x - 1,)), dma, dma((n_x - 1, n_j)), dma, dma((n_j + 1,)), dma((2,)),
                 dma((n_k,)), dma((n_k,)), dma((n_k,)), dma((n_k,)), dma((4, n_k)), dma((2,)),
-                dma((n_w,)), dma((n_w,)), dma((n_w,)), dma((n_w,)), dma((4, n_w)), dma((n_w,)),
-                dma((2 * n_x,)), dma((4, 2)), dma,
+                dma((n_w,)), dma((n_w,)), dma((n_w,)), dma((n_w,)), dma((4, n_w)), dma((2,)),
+                dma((LAG, 2 * n_x)), dma((4, n_w, 2)), dma((2,)),
             ],
             compiler_params=pltpu.CompilerParams(collective_id=0, has_side_effects=True, vmem_limit_bytes=67_043_328),
-        )(idx_loc, gate_loc, x_loc, wg_loc.reshape(d_q, ffn), wu_loc.reshape(d_q, ffn), wd_loc.reshape(ffn, d_q))
+        )(idx_loc.T, gate_loc.T, x_loc, wg_loc.reshape(d_q, ffn), wu_loc.reshape(d_q, ffn), wd_loc.reshape(ffn, d_q).T)
         return outs[0]
 
     return jax.shard_map(device_step, mesh=mesh, in_specs=(tok_spec, tok_spec, tok_spec, wide_spec, wide_spec, down_spec), out_specs=tok_spec, check_vma=False)

time: 704 us -> 531 us (0.75)
  Pallas kernels: 683 us -> 520 us
  local copies, waits for them, and re-layouts: 18.5 us -> 4.83 us
    pallas_call x1, Pallas kernels: 683 us -> 520 us  [device_step(): pl.pallas_call(functools.partial(moe_kernel, dims), name='moe_layer', out...]
    unnamed x4 -> x1, local copies, waits for them, and re-layouts: 18.5 us -> 4.83 us
where the time goes in v2:
time: 531 us; the launch traced here: 525 us
  Pallas kernels  520 us (98%)
    pallas_call x1, Pallas kernels, device_step(): pl.pallas_call(functools.partial(moe_kernel, dims), name='moe_layer', out...  520 us

profile of v2, /device:TPU:100, one launch (start us, length us, event | category | flops | bytes accessed | tf_op | source)
XLA Modules:
  0.0 525.1 jit_solution(3903092156942111671)
XLA Ops:
  0.0 520.2 %moe_layer.1 = (bf16[1024,2304]{1,0:T(8,128)(2,1)}, bf16[1024,2304]{1,0:T(8,128)(2,1)}, bf16[2560,2304]{1,0:T(8,128)(2,1)}, bf16[15,2304,768]{2,1,0:T(8,128)(2,1...) custom-call(s32[2,1024]{1,0:T(2,128)} %bitcast.10, f32[2,1024]{1,0:T(2,128)} %bitcast.11, ...), custom_call_target="tpu_custom_call" | custom-call | tf_op jit(solution)/shard_map/moe_layer/pallas_call | solution.py:542
  520.2 4.8 copy.8

commit v3 on v2

--- a/solution.py
+++ b/solution.py
@@ -10,10 +10,12 @@
 MESH = pl.DeviceIdType.MESH
 F32 = jnp.float32
 BF16 = jnp.bfloat16
-LEAD = 4
-EARLY = 11
+LEAD_FIRST = 3
+LEAD = 5
+EARLY = 13
+LATE_STEP = 4
 DOWN_STEP = 12
-LAG = 3
+STAGES = 3
 
 
 def capacity_rows(tok_rows, top_k, n_exp):
@@ -28,10 +30,11 @@
                h, keyt, keyt_par, keyc, gate_e,
                s_x, r_x, s_own, r_own, s_par, r_par, l_loc, l_x,
                s_main, s_a, s_b, s_c, r_gu, l_w,
-               t_main, t_a, t_b, t_c, r_wd, l_wd, s_ret, r_back, l_back):
-    n_x, tok, d_model, d_q, ffn, cap, fc, n_k, n_w, n_j, tile = dims
+               t_main, t_a, t_b, t_c, r_wd, l_wd, s_ret, l_ret, r_back, l_back):
+    n_x, tok, d_model, d_q, ffn, cap, fc, n_k, n_j, tile = dims
     rows = 2 * n_x * cap
-    wk = d_q // n_w
+    wk = d_q // 9 * 4
+    rest = d_q - 2 * wk
     xc = d_model // n_j
     p = lax.axis_index("expert")
     q = lax.axis_index("data")
@@ -196,12 +199,14 @@
             pass_gu(k, 1, inner_dev, s_a.at[k], 3)
             pass_gu(k, 1, partner, s_b.at[k], 1)
 
+    def part_rows(m):
+        return pl.ds(2 * wk, d_q - 2 * wk) if isinstance(m, int) and m == 2 else pl.ds(m * wk if isinstance(m, int) else pl.multiple_of(m * wk, 8), wk)
+
     def wd_rows(i, m):
-        return wdb_ref.at[quarter(i), pl.ds(pl.multiple_of(m * wk, 8), wk), :]
+        return wdb_ref.at[quarter(i), part_rows(m), :]
 
     def send_own_wd(m, device, send, recv):
-        src = wd_ref.at[pl.ds(pl.multiple_of(m * wk, 8), wk), :]
-        remote(src, wd_rows(0, m), send, recv, device).start()
+        remote(wd_ref.at[part_rows(m), :], wd_rows(0, m), send, recv, device).start()
 
     def phase_up(xr, wbuf):
         def gather_chunk(k, slot):
@@ -223,7 +228,7 @@
                 wait_for(gu_rows(k, 2), r_gu.at[2, k])
                 pltpu.make_async_copy(gu_ref.at[k], wbuf.at[slot], l_w.at[slot]).start()
 
-        for k in range(LEAD):
+        for k in range(min(LEAD_FIRST, n_k)):
             ahead(k)
 
         wait_for(xrows_ref.at[pl.ds(0, (n_x - 1) * cap), :], r_own)
@@ -247,19 +252,19 @@
         for j in range(n_j):
             wait_for(xpar_ref.at[:, pl.ds(0, xc)], s_x.at[j])
 
-        def start_wd(m, carry):
-            @pl.when(jnp.logical_not(lead))
-            def _():
+        @pl.when(lead)
+        def _():
+            for m in range(3):
+                send_own_wd(m, partner, t_a.at[m], r_wd.at[0, m])
+
+        @pl.when(jnp.logical_not(lead))
+        def _():
+            for m in range(3):
                 send_own_wd(m, outer_dev, t_main.at[m], r_wd.at[1, m])
 
-            @pl.when(lead)
-            def _():
-                send_own_wd(m, partner, t_a.at[m], r_wd.at[0, m])
-
-            return carry
-
-        lax.fori_loop(0, n_w, start_wd, 0)
         gather_chunk(0, 0)
+        for k in range(min(LEAD_FIRST, n_k), min(LEAD, n_k)):
+            ahead(k)
         load.wait()
 
         def step(k, carry):
@@ -269,17 +274,16 @@
             def _():
                 ahead(k + LEAD)
 
-            @pl.when(jnp.logical_and(lead, jnp.logical_and(k >= 2, k - 2 + early < n_k)))
-            def _():
-                send_own_gu(k - 2 + early, inner_dev, s_main.at[k - 2 + early], r_gu.at[2, k - 2 + early])
+            late = k - min(LATE_STEP, n_k - 1) + early
+
+            @pl.when(jnp.logical_and(lead, jnp.logical_and(late >= early, late < n_k)))
+            def _():
+                send_own_gu(late, inner_dev, s_main.at[late], r_gu.at[2, late])
 
             @pl.when(jnp.logical_and(k == min(DOWN_STEP, n_k - 1), lead))
             def _():
-                def start_near(m, carry2):
+                for m in range(3):
                     send_own_wd(m, inner_dev, t_main.at[m], r_wd.at[2, m])
-                    return carry2
-
-                lax.fori_loop(0, n_w, start_near, 0)
 
             @pl.when(k + 1 < n_k)
             def _():
@@ -301,11 +305,12 @@
 
     def phase_down(wdv, stage, acc, cmat, backv):
         t_tile = min(512, tok)
-        parts = 4 * n_w
         n_blocks = 2 * n_x
-
-        def ret_dst(u):
-            return back_ref.at[quarter(u // n_w), u % n_w, half, pl.ds(pl.multiple_of(cx * cap, 8), cap), :]
+        last = 8
+
+        def chunk(u, other):
+            qt = quarter(u // 2)
+            return (1 - u // last) * (2 * (qt + other * (3 - 2 * qt)) + u % 2) + u // last * last
 
         def take(i, m):
             @pl.when(jnp.logical_not(jnp.logical_and(lead, i == 0)))
@@ -314,30 +319,32 @@
 
                 @pl.when(jnp.logical_and(lead, i == 2))
                 def _():
-                    remote(wd_rows(2, m), wd_rows(2, m), t_b.at[m], r_wd.at[2, m], partner).start()
+                    remote(wd_rows(i, m), wd_rows(i, m), t_b.at[m], r_wd.at[i, m], partner).start()
 
                 @pl.when(jnp.logical_and(jnp.logical_not(lead), i == 1))
                 def _():
-                    remote(wd_rows(1, m), wd_rows(1, m), t_b.at[m], r_wd.at[1, m], partner).start()
+                    remote(wd_rows(i, m), wd_rows(i, m), t_b.at[m], r_wd.at[i, m], partner).start()
 
                 @pl.when(jnp.logical_and(jnp.logical_not(lead), i == 3))
                 def _():
-                    remote(wd_rows(3, m), wd_rows(3, m), t_c.at[m], r_wd.at[3, m], partner).start()
-
-        def load_part(u):
-            i, m = u // n_w, u % n_w
-            dst = wdv.at[lax.rem(u, 2)]
-            sem = l_wd.at[lax.rem(u, 2)]
-
+                    remote(wd_rows(i, m), wd_rows(i, m), t_c.at[m], r_wd.at[i, m], partner).start()
+
+        def load(i, m, dst, sem):
             @pl.when(jnp.logical_and(lead, i == 0))
             def _():
-                pltpu.make_async_copy(wd_ref.at[pl.ds(pl.multiple_of(m * wk, 8), wk), :], dst, sem).start()
+                pltpu.make_async_copy(wd_ref.at[part_rows(m), :], dst, sem).start()
 
             @pl.when(jnp.logical_not(jnp.logical_and(lead, i == 0)))
             def _():
                 pltpu.make_async_copy(wd_rows(i, m), dst, sem).start()
 
-        def combine(qt, m, g, add, buf):
+        def load_main(u):
+            load(u // 2, u % 2, wdv.at[u % 2], l_wd.at[u % 2])
+
+        def load_rest(i):
+            load(i, 2, wdv.at[2, pl.ds(pl.multiple_of(quarter(i) * rest, 8), rest), :], l_wd.at[2])
+
+        def combine(c, g, add, buf):
             def tok_tile(r, carry):
                 r0 = pl.multiple_of(r * t_tile, 8)
                 gates = gate_e[pl.ds(r0, t_tile), :]
@@ -349,143 +356,186 @@
                     gate_x = jnp.sum(jnp.where(lanes == e, gates, 0.0), axis=1, keepdims=True)
                     total = gate_x * rows_x if total is None else total + gate_x * rows_x
                 if add:
-                    total = total + acc[qt * n_w + m, pl.ds(r0, t_tile), :]
-                acc[qt * n_w + m, pl.ds(r0, t_tile), :] = total
+                    total = total + acc[c, pl.ds(r0, t_tile), :]
+                acc[c, pl.ds(r0, t_tile), :] = total
                 return carry
 
             lax.fori_loop(0, tok // t_tile, tok_tile, 0)
 
         def add_up(u):
-            i, m = u // n_w, u % n_w
-            here, there = quarter(i), 3 - quarter(i)
-            wait_for(back_ref.at[0, 0, 0, pl.ds(0, (n_x - 1) * cap), :], r_back.at[here, m, half])
-            first_load = pltpu.make_async_copy(back_ref.at[here, m, half], backv.at[0], l_back.at[0])
+            here, there = chunk(u, 0), chunk(u, 1)
+            wait_for(stage.at[0, 0], l_ret.at[lax.rem(u, STAGES)])
+            wait_for(back_ref.at[0, 0, pl.ds(0, (n_x - 1) * cap), :], r_back.at[here, half])
+            first_load = pltpu.make_async_copy(back_ref.at[here, half], backv.at[0], l_back.at[0])
             first_load.start()
-            wait_for(back_ref.at[0, 0, 0], r_back.at[there, m, 1 - half])
-            second_load = pltpu.make_async_copy(back_ref.at[there, m, 1 - half], backv.at[1], l_back.at[1])
+            wait_for(back_ref.at[0, 0], r_back.at[there, 1 - half])
+            second_load = pltpu.make_async_copy(back_ref.at[there, 1 - half], backv.at[1], l_back.at[1])
             second_load.start()
 
-            def both(add):
+            def both(add_first, add_second):
                 first_load.wait()
-                combine(here, m, half, add, 0)
+                combine(here, half, add_first, 0)
                 second_load.wait()
-                combine(there, m, 1 - half, add, 1)
-
-            @pl.when(i % 2 == 0)
-            def _():
-                both(False)
-
-            @pl.when(i % 2 == 1)
-            def _():
-                both(True)
-
-        take(jnp.int32(0), jnp.int32(0))
-        load_part(jnp.int32(0))
+                combine(there, 1 - half, add_second, 1)
+
+            @pl.when(jnp.logical_and(u < last, u // 2 % 2 == 0))
+            def _():
+                both(False, False)
+
+            @pl.when(jnp.logical_and(u < last, u // 2 % 2 == 1))
+            def _():
+                both(True, True)
+
+            @pl.when(u == last)
+            def _():
+                both(False, True)
 
         slot_lane = lax.broadcasted_iota(jnp.int32, (tok, cap), 1).astype(F32)
         for e in range(2 * n_x):
             cmat[e] = (slot_lane == keyc[:, e:e + 1]).astype(F32).astype(BF16)
 
+        take(0, 0)
+        load_main(0)
+
         def part(u, carry):
-            i, m = u // n_w, u % n_w
-            slot = lax.rem(u, LAG)
-
-            @pl.when(u >= 2 * n_w)
-            def _():
-                take(i, m)
-                load_part(u)
-
-            @pl.when(u == 1)
-            def _():
-                each(n_w - 2, lambda k: take(jnp.int32(0), k + 2))
-
-                @pl.when(jnp.logical_not(lead))
-                def _():
-                    each(n_w, lambda k: take(jnp.int32(1), k))
-
-            @pl.when(jnp.logical_and(u == n_w - 1, lead))
-            def _():
-                each(n_w, lambda k: take(jnp.int32(1), k))
-
-            @pl.when(jnp.logical_and(u == n_w + 1, jnp.logical_not(lead)))
-            def _():
-                each(n_w, lambda k: remote(wd_rows(1, k), wd_rows(1, k), t_a.at[k], r_wd.at[3, k], inner_dev).start())
-
-            @pl.when(jnp.logical_and(u >= 1, u + 1 < 2 * n_w))
-            def _():
-                load_part(u + 1)
-
-            wait_for(wdv.at[0], l_wd.at[lax.rem(u, 2)])
+            slot = lax.rem(u, STAGES)
+            buf = (1 - u // last) * (u % 2) + u // last * 2
+
+            @pl.when(jnp.logical_and(u >= 4, u < last))
+            def _():
+                take(u // 2, u % 2)
+                load_main(u)
+
+            @pl.when(u == 0)
+            def _():
+                take(0, 1)
+                load_main(u + 1)
+                take(0, 2)
+                load_rest(0)
+
+            @pl.when(jnp.logical_and(u == 1, jnp.logical_not(lead)))
+            def _():
+                for m in range(3):
+                    take(1, m)
+                for m in range(3):
+                    remote(wd_rows(1, m), wd_rows(1, m), t_a.at[m], r_wd.at[3, m], inner_dev).start()
+
+            @pl.when(jnp.logical_and(u == 1, lead))
+            def _():
+                for m in range(3):
+                    take(1, m)
+
+            @pl.when(jnp.logical_and(u >= 1, u <= 2))
+            def _():
+                load_main(u + 1)
+
+            @pl.when(u == 2)
+            def _():
+                load_rest(1)
+
+            @pl.when(u == 6)
+            def _():
+                take(2, 2)
+                load_rest(2)
+
+            @pl.when(u < last)
+            def _():
+                wait_for(wdv.at[0], l_wd.at[u % 2])
+
+            @pl.when(u == last)
+            def _():
+                load_rest(3)
+                wait_for(wdv.at[2], l_wd.at[2])
 
             def block(t, carry2):
                 s = (t // n_x + 1 - cc) % 2
                 x_src = lax.rem(cx + 1 + t % n_x, n_x)
                 r0 = pl.multiple_of((x_src * 2 + s) * cap, 8)
-                out = lax.dot_general(h[pl.ds(r0, cap), :], wdv[lax.rem(u, 2)], (((1,), (1,)), ((), ())), preferred_element_type=F32)
-
-                @pl.when(u >= LAG)
+                local = jnp.logical_and(s == 0, t % n_x == n_x - 1)
+
+                @pl.when(jnp.logical_and(u == last - 1, t == n_x))
+                def _():
+                    take(3, 2)
+
+                out = lax.dot_general(h[pl.ds(r0, cap), :], wdv[buf], (((1,), (1,)), ((), ())), preferred_element_type=F32)
+
+                @pl.when(jnp.logical_and(u >= STAGES, jnp.logical_not(local)))
                 def _():
                     wait_for(stage.at[0, 0], s_ret.at[slot, t])
 
                 stage[slot, t] = out.astype(BF16)
-                local = jnp.logical_and(s == 0, t % n_x == n_x - 1)
+                dst = back_ref.at[chunk(u, 0), half, pl.ds(pl.multiple_of(cx * cap, 8), cap), :]
 
                 @pl.when(jnp.logical_not(local))
                 def _():
-                    remote(stage.at[slot, t], ret_dst(u), s_ret.at[slot, t], r_back.at[quarter(i), m, half], dev(x_src, q + s * (outer - q), cc)).start()
+                    remote(stage.at[slot, t], dst, s_ret.at[slot, t], r_back.at[chunk(u, 0), half], dev(x_src, q + s * (outer - q), cc)).start()
 
                 @pl.when(local)
                 def _():
-                    pltpu.make_async_copy(stage.at[slot, t], ret_dst(u), s_ret.at[slot, t]).start()
+                    pltpu.make_async_copy(stage.at[slot, t], dst, l_ret.at[slot]).start()
 
                 return carry2
 
             lax.fori_loop(0, n_blocks, block, 0)
 
-            @pl.when(u == 0)
-            def _():
-                take(0, jnp.int32(1))
-                load_part(jnp.int32(1))
-
-            @pl.when(u >= LAG)
-            def _():
-                add_up(u - LAG)
+            def adds(v, carry2):
+                add_up(v)
+                return carry2
+
+            @pl.when(jnp.logical_and(u >= 2, u < last - 1))
+            def _():
+                lax.fori_loop(u - 2, u - 1 + u // 6, adds, 0)
 
             return carry
 
-        lax.fori_loop(0, parts, part, 0)
+        lax.fori_loop(0, last + 1, part, 0)
 
         x_here = h.at[pl.ds(0, tok), pl.ds(0, d_model)]
-        load = pltpu.make_async_copy(x_ref, x_here, l_x.at[0])
-        load.start()
-
-        def rest(k):
-            u = parts - LAG + k
-            each(n_blocks, lambda t: wait_for(stage.at[0, 0], s_ret.at[lax.rem(u, LAG), t]))
-            add_up(u)
-
-        each(LAG, rest)
-        load.wait()
+        x_load = pltpu.make_async_copy(x_ref, x_here, l_x.at[0])
+        x_load.start()
+        each(last - 5, lambda k: add_up(k + 6))
+        x_load.wait()
 
         def finish(r, carry):
             r0 = pl.multiple_of(r * t_tile, 8)
-            for c in range(4 * n_w):
-                cols = pl.ds(c * wk, wk)
-                total = h[pl.ds(r0, t_tile), cols].astype(F32) + acc[c, pl.ds(r0, t_tile), :]
-                h[pl.ds(r0, t_tile), cols] = total.astype(BF16)
+
+            def put(c0, width, extra):
+                cols = pl.ds(c0, width)
+                h[pl.ds(r0, t_tile), cols] = (h[pl.ds(r0, t_tile), cols].astype(F32) + extra).astype(BF16)
+
+            for qt in range(4):
+                for m in range(2):
+                    put(qt * d_q + m * wk, wk, acc[2 * qt + m, pl.ds(r0, t_tile), :])
+                put(qt * d_q + 2 * wk, rest, acc[last, pl.ds(r0, t_tile), pl.ds(qt * rest, rest)])
             return carry
 
         lax.fori_loop(0, tok // t_tile, finish, 0)
         store = pltpu.make_async_copy(x_here, y_ref, l_x.at[0])
         store.start()
+
+        def sent(k, carry):
+            u = last - STAGES + 1 + k
+
+            def sent_block(t, carry2):
+                s = (t // n_x + 1 - cc) % 2
+
+                @pl.when(jnp.logical_not(jnp.logical_and(s == 0, t % n_x == n_x - 1)))
+                def _():
+                    wait_for(stage.at[0, 0], s_ret.at[lax.rem(u, STAGES), t])
+
+                return carry2
+
+            return lax.fori_loop(0, n_blocks, sent_block, carry)
+
+        lax.fori_loop(0, STAGES, sent, 0)
         store.wait()
 
     pl.run_scoped(phase_up, pltpu.VMEM((rows, d_model), BF16), pltpu.VMEM((2, d_model, 2 * fc), BF16))
     pl.run_scoped(
         phase_down,
-        pltpu.VMEM((2, wk, ffn), BF16),
-        pltpu.VMEM((LAG, 2 * n_x, cap, wk), BF16),
-        pltpu.VMEM((4 * n_w, tok, wk), F32),
+        pltpu.VMEM((3, wk, ffn), BF16),
+        pltpu.VMEM((STAGES, 2 * n_x, cap, wk), BF16),
+        pltpu.VMEM((9, tok, wk), F32),
         pltpu.VMEM((2 * n_x, tok, cap), BF16),
         pltpu.VMEM((2, n_x * cap, wk), BF16),
     )
@@ -503,18 +553,14 @@
 
     lax.fori_loop(0, n_k, drain_gu, 0)
 
-    def drain_wd(m, carry):
-        wait_for(wd_rows(0, m), t_main.at[m])
-        wait_for(wd_rows(0, m), t_a.at[m])
-        wait_for(wd_rows(0, m), t_b.at[m])
-
-        @pl.when(jnp.logical_not(lead))
-        def _():
+    for m in range(3):
+        for sem in (t_main, t_a, t_b):
+            wait_for(wd_rows(0, m), sem.at[m])
+
+    @pl.when(jnp.logical_not(lead))
+    def _():
+        for m in range(3):
             wait_for(wd_rows(0, m), t_c.at[m])
-
-        return carry
-
-    lax.fori_loop(0, n_w, drain_wd, 0)
 
 
 def solution(mesh):
@@ -528,13 +574,13 @@
     def device_step(x_loc, idx_loc, gate_loc, wg_loc, wu_loc, wd_loc):
         tok, d_model = x_loc.shape
         n_local, d_q, ffn = wg_loc.shape
-        assert n_local == 1 and n_group == 8
+        assert n_local == 1 and n_group == 8 and d_q % 72 == 0
         cap = capacity_rows(tok, idx_loc.shape[1], n_group)
         fc = pick(ffn, (384, 256, 128))
-        n_k, n_w, n_j = ffn // fc, pick(d_q // 8, (3, 2, 1)), pick(d_model // 128, (3, 2, 1))
+        n_k, n_j = ffn // fc, pick(d_model // 128, (3, 2, 1))
         rows = 2 * n_x * cap
         tile = pick(rows, (640, 48, 8))
-        dims = (n_x, tok, d_model, d_q, ffn, cap, fc, n_k, n_w, n_j, tile)
+        dims = (n_x, tok, d_model, d_q, ffn, cap, fc, n_k, n_j, tile)
         hbm = pl.BlockSpec(memory_space=pl.ANY)
         vmem = pl.BlockSpec(memory_space=pltpu.VMEM)
         dma = pltpu.SemaphoreType.DMA
@@ -548,7 +594,7 @@
                 shape((rows, d_model), BF16),
                 shape((n_k, d_model, 2 * fc), BF16),
                 shape((4, d_q, ffn), BF16),
-                shape((4, n_w, 2, n_x * cap, d_q // n_w), BF16),
+                shape((9, 2, n_x * cap, d_q // 9 * 4), BF16),
             ],
             in_specs=[vmem, vmem, hbm, hbm, hbm, hbm],
             out_specs=[hbm] * 6,
@@ -560,8 +606,8 @@
                 pltpu.VMEM((tok, 128), F32),
                 dma((n_j + 1,)), dma((n_j + 1,)), dma((n_x - 1,)), dma, dma((n_x - 1, n_j)), dma, dma((n_j + 1,)), dma((2,)),
                 dma((n_k,)), dma((n_k,)), dma((n_k,)), dma((n_k,)), dma((4, n_k)), dma((2,)),
-                dma((n_w,)), dma((n_w,)), dma((n_w,)), dma((n_w,)), dma((4, n_w)), dma((2,)),
-                dma((LAG, 2 * n_x)), dma((4, n_w, 2)), dma((2,)),
+                dma((3,)), dma((3,)), dma((3,)), dma((3,)), dma((4, 3)), dma((3,)),
+                dma((STAGES, 2 * n_x)), dma((STAGES,)), dma((9, 2)), dma((2,)),
             ],
             compiler_params=pltpu.CompilerParams(collective_id=0, has_side_effects=True, vmem_limit_bytes=67_043_328),
         )(idx_loc.T, gate_loc.T, x_loc, wg_loc.reshape(d_q, ffn), wu_loc.reshape(d_q, ffn), wd_loc.reshape(ffn, d_q).T)

time: 531 us -> 499 us (0.940)
  Pallas kernels: 520 us -> 494 us
    pallas_call x1, Pallas kernels: 520 us -> 494 us  [device_step(): pl.pallas_call(functools.partial(moe_kernel, dims), name='moe_layer', out...]
where the time goes in v3:
time: 499 us; the launch traced here: 498 us
  Pallas kernels  494 us (99%)
    pallas_call x1, Pallas kernels, device_step(): pl.pallas_call(functools.partial(moe_kernel, dims), name='moe_layer', out...  494 us

profile of v3, /device:TPU:100, one launch (start us, length us, event | category | flops | bytes accessed | tf_op | source)
XLA Modules:
  0.0 498.3 jit_solution(11051457092141020765)
XLA Ops:
  0.0 493.5 %moe_layer.1 = (bf16[1024,2304]{1,0:T(8,128)(2,1)}, bf16[1024,2304]{1,0:T(8,128)(2,1)}, bf16[2560,2304]{1,0:T(8,128)(2,1)}, bf16[15,2304,768]{2,1,0:T(8,128)(2,1...) custom-call(s32[2,1024]{1,0:T(2,128)} %bitcast.10, f32[2,1024]{1,0:T(2,128)} %bitcast.11, ...), custom_call_target="tpu_custom_call" | custom-call | tf_op jit(solution)/shard_map/moe_layer/pallas_call | solution.py:588
  493.5 4.8 copy.8
